TPU v7x, 32 devices: a 4x2x2 block of a 4x4x8 slice. The times are simulated.
32 devices in a mesh: data: 4 (over y, z), dap: 8 (over x, core).
Axes of the slice: x: 4, y: 2, z: 2, core: 2. Of those that a mesh axis runs over, the one named last changes fastest.
The devices are a block of a 4x4x8 slice.
Arguments:
- msa_act: bfloat16 [1024, 64, 256], P(('data', 'dap')), parts along dimension 0
- pair_act: bfloat16 [256, 64, 128], P(('data', 'dap')), parts along dimension 0
- msa_mask: int32 [1024, 64], P('data'), parts along dimension 0
- res_mask: int32 [256], P('data'), parts along dimension 0
- w_row_bias: bfloat16 [2, 128, 8], replicated
- w_row_in: bfloat16 [2, 256, 4, 8, 32], replicated
- w_row_out: bfloat16 [2, 8, 32, 256], replicated
- w_col_in: bfloat16 [2, 256, 4, 8, 32], replicated
- w_col_out: bfloat16 [2, 8, 32, 256], replicated
- w_opm_in: bfloat16 [2, 256, 2, 32], replicated
- w_opm_out: bfloat16 [2, 32, 32, 128], replicated
- w_ts_bias: bfloat16 [2, 128, 4], replicated
- w_ts_in: bfloat16 [2, 128, 4, 4, 32], replicated
- w_ts_out: bfloat16 [2, 4, 32, 128], replicated
- w_te_bias: bfloat16 [2, 128, 4], replicated
- w_te_in: bfloat16 [2, 128, 4, 4, 32], replicated
- w_te_out: bfloat16 [2, 4, 32, 128], replicated
Outputs:
- output 1: bfloat16 [1024, 64, 256], P(('data', 'dap')), parts along dimension 0
- output 2: bfloat16 [256, 64, 128], P(('data', 'dap')), parts along dimension 0
There are 4 independent parts. A program takes and returns all parts, laid end to end along the dimension named above; an argument that names none is the same for every part.
All inputs are finite; a program needn't handle non-finite values.
Results may differ from a plain program's by a relative error of at most 0.0181275.
Values are sent between devices in bfloat16 or wider.
A program may use at most 768 MiB of HBM per device.

v0:
```python
import functools
import math

import jax
import jax.numpy as jnp
from jax import lax
from jax.experimental import pallas as pl
from jax.experimental.pallas import tpu as pltpu
from jax.sharding import PartitionSpec as P

F32 = jnp.float32
BF16 = jnp.bfloat16
VMEM = pltpu.VMEM
HEAD = 32
RES = 2 * HEAD
LANE = 2 * RES
SEQ = 2 * LANE
WIDE = 4 * SEQ
OWN = 8
BLK = 16
LOG2E = math.log2(math.e)
NEG = -1e9 * LOG2E
SCALE = HEAD ** -0.5 * LOG2E


def dot_nn(a, b):
    return lax.dot_general(a, b, (((1,), (0,)), ((), ())), preferred_element_type=F32)


def dot_nt(a, b):
    return lax.dot_general(a, b, (((1,), (1,)), ((), ())), preferred_element_type=F32)


def dot_tn(a, b):
    return lax.dot_general(a, b, (((0,), (0,)), ((), ())), preferred_element_type=F32)


def iota(shape, axis):
    return lax.broadcasted_iota(jnp.int32, shape, axis)


def selector(rows, cols, source):
    return jnp.where(iota((rows, cols), 1) == source(iota((rows, cols), 0)), 1.0, 0.0).astype(BF16)


def rounded(x):
    return x.astype(BF16).astype(F32)


def layer_norm(x):
    scale = 1.0 / x.shape[-1]
    mean = jnp.sum(x, axis=-1, keepdims=True) * scale
    cen = x - mean
    var = jnp.sum(cen * cen, axis=-1, keepdims=True) * scale
    return (cen * lax.rsqrt(var + 1e-5)).astype(BF16)


def column(values, index):
    return jnp.sum(jnp.where(iota(values.shape, 1) == index, values, 0.0), axis=1, keepdims=True)


def softmax_rows(t):
    e = jnp.exp2(t - jnp.max(t, axis=0, keepdims=True))
    return (e * (1.0 / jnp.sum(e, axis=0, keepdims=True))).astype(BF16)


def interleave(*gens):
    gens = list(gens)
    while gens:
        for gen in list(gens):
            try:
                next(gen)
            except StopIteration:
                gens.remove(gen)


def project(load, w, bufs):
    q, k, v, g, _ = bufs
    hd = k.shape[1]
    x = layer_norm(load())
    yield
    q[...] = rounded(dot_nt(w[0:hd], x)).astype(q.dtype)
    yield
    k[...] = dot_nt(x, w[hd:2 * hd]).astype(BF16)
    yield
    v[...] = dot_nt(w[2 * hd:3 * hd], x).astype(BF16)
    yield
    g[...] = jax.nn.sigmoid(rounded(dot_nt(w[3 * hd:4 * hd], x)))
    yield


def col_attend(bufs, keep, ahead=2, late=1):
    q, k, v, g, o = bufs
    heads, length = q.shape[0] // HEAD, q.shape[1]
    per = LANE // HEAD

    def logits(h):
        r = h % per
        parts = [jnp.zeros((HEAD * r, length), BF16)] if r else []
        parts.append(q[h * HEAD:(h + 1) * HEAD, :])
        if r < per - 1:
            parts.append(jnp.zeros((HEAD * (per - 1 - r), length), BF16))
        lanes = slice(h // per * LANE, (h // per + 1) * LANE)
        return dot_nn(k[:, lanes], jnp.concatenate(parts, axis=0))

    pend = {i: logits(i) for i in range(ahead)}
    probs = {}
    for i in range(heads + late):
        if i + ahead < heads:
            pend[i + ahead] = logits(i + ahead)
        if i >= late:
            rows = slice((i - late) * HEAD, (i - late + 1) * HEAD)
            o[rows, :] = (dot_nn(v[rows, :], probs.pop(i - late)) * g[rows, :]).astype(BF16)
        if i < heads:
            probs[i] = softmax_rows(jnp.where(keep, pend.pop(i) * SCALE, NEG))
        yield


def row_attend(bufs, bias, masks, ahead=4, late=2):
    q, k, v, g, o = bufs
    groups = q.shape[0] // LANE
    low = iota((HEAD, LANE), 1) < RES
    zero = jnp.zeros((RES, LANE), BF16)

    def diag(a, b):
        return jnp.concatenate([jnp.concatenate([a, zero], axis=1), jnp.concatenate([zero, b], axis=1)], axis=0)

    def logits(pair, group, s):
        lanes = slice(pair * LANE, (pair + 1) * LANE)
        halves = []
        for t in range(2):
            h0 = group * LANE + t * RES
            even, odd = q[h0:h0 + HEAD, lanes], q[h0 + HEAD:h0 + RES, lanes]
            if s:
                even = pltpu.roll(even, RES, 1)
            else:
                odd = pltpu.roll(odd, RES, 1)
            halves.append(jnp.concatenate([jnp.where(low, even, 0.0), jnp.where(low, 0.0, odd)], axis=0).astype(BF16))
        r0 = (pair * 2 + s) * RES
        return dot_nn(k[r0:r0 + RES, group * LANE:(group + 1) * LANE], diag(*halves))

    def weighted(pair, group):
        lanes = slice(pair * LANE, (pair + 1) * LANE)
        first, second = probs.pop((pair, group, 0)), probs.pop((pair, group, 1))
        for t in range(2):
            part = slice(t * LANE, (t + 1) * LANE)
            rows = slice(group * LANE + t * RES, group * LANE + (t + 1) * RES)
            both = dot_nn(v[rows, lanes], diag(first[:, part], second[:, part]))
            b0, b1 = both[:, :LANE], both[:, LANE:]
            out = jnp.concatenate([jnp.where(low, b0[:HEAD], pltpu.roll(b1[:HEAD], RES, 1)),
                                   jnp.where(low, pltpu.roll(b0[HEAD:], RES, 1), b1[HEAD:])], axis=0)
            o[rows, lanes] = (out * g[rows, lanes]).astype(BF16)

    units = [(pair, group, s) for pair in range(2) for group in range(groups) for s in range(2)]
    pend = {u: logits(*u) for u in units[:ahead]}
    probs = {}
    for i in range(len(units) + late):
        if i + ahead < len(units):
            pend[units[i + ahead]] = logits(*units[i + ahead])
        if i >= late and units[i - late][2]:
            weighted(*units[i - late][:2])
        if i < len(units):
            pair, group, s = units[i]
            t = pend.pop(units[i]) * SCALE + bias[:, group * SEQ:(group + 1) * SEQ]
            probs[units[i]] = softmax_rows(jnp.where(masks[pair * 2 + s] > 0.5, t, NEG))
        yield


def kernel(n, m_ref, z_ref, mask_ref, res_ref,
           wrb_ref, wri_ref, wro_ref, wci_ref, wco_ref, woi_ref, woo_ref,
           wsb_ref, wsi_ref, wso_ref, web_ref, wei_ref, weo_ref,
           mo_ref, zo_ref,
           mf, zf, mcol, mrow, send_m, send_b, slot_b, bias_r, bias_t, mask_t, mask_n, rnorm, res_col,
           swap, rot, perm_s, perm_r, opm_rhs, opm_stage, opm_send, opm_all, opm_lhs, opm_w, opm_w4, opm_f, opm_t,
           send_z, slot_z,
           cq, ck, cv, cg, co, rq, rk, rv, rg, ro, tq, tk, tv, tg, to,
           ss_b, rs_b, ss_m, rs_m, ss_c, rs_c, ss_r, rs_r, ss_z, rs_z):
    me = lax.axis_index('dap')
    peers = [lax.rem(me + off, n) for off in range(1, n)]
    partner = me + 1 - 2 * lax.rem(me, 2)
    others = [lax.rem(me + off, n) for off in range(2, n, 2)]
    scope = jax.named_scope

    def remote(src, dst, send_sem, recv_sem, peer):
        return pltpu.make_async_remote_copy(src_ref=src, dst_ref=dst, send_sem=send_sem, recv_sem=recv_sem,
                                            device_id={'dap': peer}, device_id_type=pl.DeviceIdType.MESH)

    with scope('barrier'):
        barrier = pltpu.get_barrier_semaphore()
        for peer in peers:
            pl.semaphore_signal(barrier, inc=1, device_id={'dap': peer}, device_id_type=pl.DeviceIdType.MESH)
        pl.semaphore_wait(barrier, n - 1)

    def bias_send(idx, w_bias, heads):
        z_cat = jnp.concatenate([layer_norm(zf[l]) for l in range(OWN)], axis=1)
        w = w_bias.astype(F32)
        w_rows = jnp.concatenate([jnp.broadcast_to(w[h:h + 1], (OWN, LANE)) for h in range(heads)], axis=0)
        own = iota(w_rows.shape, 0) % OWN
        lhs = jnp.concatenate([jnp.where(own == l, w_rows, 0.0).astype(BF16) for l in range(OWN)], axis=1)
        part = dot_nt(lhs, jnp.concatenate([z_cat, z_cat], axis=0))
        if heads < OWN:
            part = jnp.concatenate([part, jnp.zeros((RES - part.shape[0], LANE), F32)], axis=0)
        part = part.astype(BF16)
        send_b[idx] = part
        slot_b[idx, me] = part
        for j, peer in enumerate(peers):
            remote(send_b.at[idx], slot_b.at[idx, me], ss_b.at[idx, j], rs_b.at[idx, me], peer).start()

    def bias_slots(idx):
        with scope('bias_wait'):
            for j, src in enumerate(peers):
                c = remote(send_b.at[idx], slot_b.at[idx, src], ss_b.at[idx, j], rs_b.at[idx, src], src)
                c.wait_send()
                c.wait_recv()
        return jnp.concatenate([slot_b[idx, d] for d in range(n)], axis=0)

    def bias_query_local(idx, heads, out):
        full = dot_tn(bias_slots(idx), swap[:, :heads * RES])
        out[...] = full[:RES] * LOG2E

    def bias_key_local(idx, out):
        full = dot_nn(swap[...], bias_slots(idx)) * LOG2E
        low = iota((RES, LANE), 1) < RES
        for t in range(OWN // 2):
            lanes = slice(t * LANE, (t + 1) * LANE)
            out[:, lanes] = jnp.where(low, full[lanes][:RES], full[lanes][RES:])

    row_bufs = lambda s: [buf.at[s] for buf in (rq, rk, rv, rg, ro)]

    def row_pass(b, load, store, first, count, hook):
        interleave(project(lambda: load(first), wri_ref.at[b], row_bufs(0)))
        ro[1] = jnp.zeros(ro.shape[1:], BF16)

        def finish(grp, slot, to):
            yield
            upd = dot_tn(ro[slot], wro_ref[b])
            yield
            store(to, rounded(load(grp) + upd).reshape(4, RES, SEQ))
            yield

        def body(step, carry):
            grp = first + step
            s = lax.rem(step, 2)
            masks = [column(mask_t[...], me * HEAD + grp * 4 + j) for j in range(4)]
            interleave(row_attend(row_bufs(s), bias_r, masks),
                       project(lambda: load(jnp.minimum(grp + 1, first + count - 1)), wri_ref.at[b], row_bufs(1 - s)),
                       finish(jnp.maximum(grp - 1, first), 1 - s, jnp.where(step == 0, OWN, grp - 1)))
            hook(step)
            return carry
        lax.fori_loop(0, count, body, 0)
        interleave(finish(first + count - 1, (count - 1) % 2, first + count - 1))

    def triangle(idx, w_in, w_out):
        bias_query_local(idx, 4, bias_t)
        with scope('tri'):
            masks = [res_col[:, 0:1]] * 4
            bufs = [[buf.at[c] for buf in (tq, tk, tv, tg, to)] for c in range(2)]
            load = [lambda c=c: zf[c * 4:(c + 1) * 4].reshape(SEQ, LANE) for c in range(2)]

            def finish(c):
                yield
                upd = dot_tn(to[c], w_out)
                yield
                zf[c * 4:(c + 1) * 4] = rounded(load[c]() + upd).reshape(4, RES, LANE)
            interleave(project(load[0], w_in, bufs[0]), project(load[1], w_in, bufs[1]))
            interleave(row_attend(bufs[0], bias_t, masks), row_attend(bufs[1], bias_t, masks))
            interleave(finish(0), finish(1))

    def z_send(idx):
        out = dot_nn(swap[...], zf[...].reshape(OWN * RES, LANE).astype(BF16)).astype(BF16)
        for d in range(n):
            send_z[idx, d] = out[d * RES:(d + 1) * RES]
        slot_z[idx, me] = send_z[idx, me]
        for j, peer in enumerate(peers):
            remote(send_z.at[idx, peer], slot_z.at[idx, me], ss_z.at[idx, j], rs_z.at[idx, me], peer).start()

    def z_recv(idx):
        with scope('z_wait'):
            for j, peer in enumerate(peers):
                c = remote(send_z.at[idx, peer], slot_z.at[idx, peer], ss_z.at[idx, j], rs_z.at[idx, peer], peer)
                c.wait_send()
                c.wait_recv()
        zf[...] = dot_nn(rot[...], jnp.concatenate([slot_z[idx, d] for d in range(n)], axis=0)).reshape(OWN, RES, LANE)

    def opm_start(b):
        out = dot_nn(selector(RES, RES, lambda r: r % OWN * OWN + r // OWN), opm_stage[0:RES].astype(BF16)).astype(BF16)
        opm_send[b] = out
        opm_all[b, me] = out
        for j, peer in enumerate([partner] + others):
            remote(opm_send.at[b], opm_all.at[b, me], ss_c.at[b, j], rs_c.at[b, me], peer).start()

    def opm_forward(b):
        with scope('opm_fwd'):
            for j, src in enumerate(others):
                remote(opm_all.at[b, src], opm_all.at[b, src], ss_c.at[b, len(others) + 1 + j], rs_c.at[b, src], partner).wait_recv()
                remote(opm_all.at[b, src], opm_all.at[b, src], ss_c.at[b, len(others) + 1 + j], rs_c.at[b, src], partner).start()

    def opm_finish(b, w_out):
        with scope('opm_wait'):
            for src in [partner] + [partner_of(o) for o in others]:
                remote(opm_send.at[b], opm_all.at[b, src], ss_c.at[b, 0], rs_c.at[b, src], partner).wait_recv()
            for j in range(n - 1):
                remote(opm_send.at[b], opm_all.at[b, me], ss_c.at[b, j], rs_c.at[b, me], partner).wait_send()
        with scope('opm'):
            lhs = opm_all[b].reshape(OWN * RES, WIDE)
            for pair in range(OWN // 2):
                part = rounded(dot_nn(lhs, opm_rhs[b, pair])).reshape(n, OWN, OWN, SEQ)
                for g in range(OWN):
                    rows = part[:, g].reshape(RES, SEQ)
                    for half in range(2):
                        l = pair * 2 + half
                        opm_lhs[l * RES:(l + 1) * RES, g * LANE:(g + 1) * LANE] = rows[:, half * LANE:(half + 1) * LANE]
            upd = dot_nn(opm_lhs[...].astype(BF16), w_out).reshape(OWN, RES, LANE)
            zf[...] = rounded(zf[...] + upd * rnorm[...])

    def partner_of(dev):
        return dev + 1 - 2 * lax.rem(dev, 2)

    zf[...] = z_ref[...].astype(F32)
    with scope('bias0'):
        bias_send(0, wrb_ref[0], OWN)

    with scope('consts'):
        flat = OWN * RES
        swap[...] = selector(flat, flat, lambda r: r // OWN % OWN * RES + r // RES * OWN + r % OWN)
        rot[...] = selector(flat, flat, lambda r: r // OWN % OWN * RES + r % OWN * OWN + r // RES)
        perm_s[...] = selector(LANE, LANE, lambda r: r % BLK * OWN + r // BLK)
        perm_r[...] = selector(SEQ, SEQ, lambda r: r % OWN * HEAD + r // OWN)
        m_t = mask_ref[...].astype(F32)
        mask_t[...] = m_t
        mask_n[...] = m_t.T
        norm = dot_nt(m_t.astype(BF16), m_t.astype(BF16))
        for l in range(OWN):
            rnorm[l] = jnp.broadcast_to(1.0 / (1e-3 + column(norm, me * OWN + l)), (RES, LANE))
        res = jnp.broadcast_to(res_ref[...].astype(F32), (RES, RES))
        eye = iota(res.shape, 0) == iota(res.shape, 1)
        res_col[...] = jnp.broadcast_to(jnp.sum(jnp.where(eye, res, 0.0), axis=1, keepdims=True), res_col.shape)
        spread = selector(HEAD, HEAD, lambda r: r % OWN * 4 + r // OWN)
        for b in range(2):
            a, c = woi_ref[b, 0:HEAD], woi_ref[b, HEAD:RES]
            gat, loc = (c, a) if b == 0 else (a, c)
            opm_w[b] = dot_nn(spread, gat).astype(BF16)
            opm_w4[b] = jnp.concatenate([loc] * 4, axis=0)
        opm_f[...] = woo_ref[0].astype(F32)
        for r in range(HEAD):
            opm_t[r * HEAD:(r + 1) * HEAD] = opm_f[pl.ds(r, HEAD, stride=HEAD), :].astype(BF16)
        co[1] = jnp.zeros(co.shape[1:], BF16)

    bias_query_local(0, OWN, bias_r)

    def send_chunk(chunk):
        rows = slice(chunk * BLK, (chunk + 1) * BLK)
        for off in range(n):
            dst = me if off == 0 else peers[off - 1]
            blk = mf[rows, pl.ds(pl.multiple_of(dst * OWN, OWN), OWN), :].reshape(LANE, SEQ).astype(BF16)
            blk = dot_nn(perm_s[...], blk).astype(BF16).reshape(OWN, BLK, SEQ)
            if off == 0:
                mcol[0:OWN, me * 2 + chunk] = blk
            else:
                send_m[chunk, off - 1] = blk
        for i in range(OWN):
            for j, peer in enumerate(peers):
                remote(send_m.at[chunk, j, i], mcol.at[i, me * 2 + chunk], ss_m.at[chunk], rs_m.at[chunk, i], peer).start()

    def load_first(grp):
        return m_ref[pl.ds(grp * 4, 4)].reshape(SEQ, SEQ).astype(F32)

    def store_first(grp, value):
        mf[pl.ds(grp * 4, 4)] = value

    for chunk in range(2):
        with scope('row1'):
            row_pass(0, load_first, store_first, chunk * 4, 4, lambda step: None)
        with scope('send_chunk'):
            send_chunk(chunk)

    col_bufs = lambda s: [buf.at[s] for buf in (cq, ck, cv, cg, co)]

    def residue_wait(i):
        for chunk in range(2):
            seven = send_m.at[chunk, :, 0]
            pltpu.make_async_copy(seven, seven, rs_m.at[chunk, i]).wait()

    def load_col(i):
        return mcol[i].reshape(SEQ, SEQ).astype(F32)

    def col_finish(b, i, slot):
        safe = jnp.minimum(i, OWN - 1)
        yield
        upd = dot_tn(co[slot], wco_ref[b])
        yield
        x = rounded(load_col(i) + upd)
        mcol[i] = x.astype(BF16).reshape(BLK, BLK, SEQ)
        x = layer_norm(x)
        yield
        local = (dot_nt(x, opm_w4[b]) * column(mask_n[...], me * OWN + safe)).astype(BF16)
        part = iota(local.shape, 1) // HEAD
        lanes = pl.ds(pl.multiple_of(lax.rem(i, 2) * LANE, LANE), LANE)
        for r in range(4):
            opm_rhs[b, lax.div(i, 2), r * SEQ:(r + 1) * SEQ, lanes] = jnp.where(part == r, local, jnp.zeros_like(local))
        yield
        gathered = rounded(dot_nt(opm_w[b], x) * mask_t[pl.ds(me * OWN + safe, 1), :])
        for r in range(4):
            opm_stage[pl.ds(pl.multiple_of(i * OWN, OWN), OWN), r * SEQ:(r + 1) * SEQ] = gathered[r * OWN:(r + 1) * OWN]
        yield

    def send_back(i):
        mrow[me, i] = mcol[i, pl.ds(me * 2, 2)]
        for j, peer in enumerate(peers):
            remote(mcol.at[i, pl.ds(peer * 2, 2)], mrow.at[me, i], ss_r.at[j], rs_r.at[me], peer).start()

    with scope('col_first'):
        residue_wait(0)
        interleave(project(lambda: load_col(0), wci_ref.at[0], col_bufs(0)))

    def at(step, when, fn):
        @pl.when(step == when)
        def _():
            fn()

    def stage_opm():
        opm_finish(0, opm_t[...])
        bias_send(1, wsb_ref[0], 4)

    def stage_start():
        triangle(1, wsi_ref.at[0], wso_ref[0])
        z_send(0)

    def stage_turn():
        z_recv(0)
        bias_send(2, web_ref[0], 4)

    def col_body(step, carry):
        @pl.when(step < OWN - 1)
        def _():
            residue_wait(step + 1)
        with scope('col'):
            s = lax.rem(step, 2)
            keep = column(mask_n[...], me * OWN + lax.rem(step, OWN)) > 0.5
            nxt, prev = step + 1, step - 1
            interleave(
                col_attend(col_bufs(s), keep),
                project(lambda: load_col(lax.rem(nxt, OWN)), wci_ref.at[jnp.minimum(lax.div(nxt, OWN), 1)], col_bufs(1 - s)),
                col_finish(jnp.where(prev >= OWN, 1, 0), jnp.where(step == 0, OWN, lax.rem(jnp.maximum(prev, 0), OWN)), 1 - s))

        @pl.when(prev >= OWN)
        def _():
            send_back(prev - OWN)
        at(step, OWN, lambda: opm_start(0))
        at(step, OWN + 2, lambda: opm_forward(0))
        at(step, OWN + 3, stage_opm)
        at(step, OWN + 5, stage_start)
        at(step, OWN + 7, stage_turn)
        return carry
    lax.fori_loop(0, 2 * OWN, col_body, 0)
    with scope('col_last'):
        interleave(col_finish(1, OWN - 1, 1))
        send_back(OWN - 1)

    triangle(2, wei_ref.at[0], weo_ref[0])
    with scope('bias3'):
        bias_send(3, wrb_ref[1], OWN)
        opm_start(1)

    with scope('m_wait'):
        for chunk in range(2):
            sent = send_m.at[chunk]
            pltpu.make_async_copy(sent, sent, ss_m.at[chunk]).wait()
        for j, src in enumerate(peers):
            pltpu.make_async_copy(mrow.at[src], mrow.at[src], rs_r.at[src]).wait()
            pltpu.make_async_copy(mrow.at[src], mrow.at[src], ss_r.at[j]).wait()
    with scope('m_perm'):
        for d in range(n):
            mf[0:HEAD, d * OWN:(d + 1) * OWN, :] = dot_nn(perm_r[...], mrow[d].reshape(SEQ, SEQ)).reshape(HEAD, OWN, SEQ)
    bias_key_local(3, bias_r)

    def stage_opm2():
        opm_finish(1, woo_ref[1])
        bias_send(4, web_ref[1], 4)

    def stage_end2():
        triangle(4, wei_ref.at[1], weo_ref[1])
        z_send(1)

    def stage_turn2():
        z_recv(1)
        bias_send(5, wsb_ref[1], 4)

    def row_hook(step):
        at(step, 2, lambda: opm_forward(1))
        at(step, 3, stage_opm2)
        at(step, 5, stage_end2)
        at(step, 7, stage_turn2)

    def load_second(grp):
        return mf[pl.ds(grp * 4, 4)].reshape(SEQ, SEQ)

    with scope('row2'):
        row_pass(1, load_second, store_first, 0, OWN, row_hook)
    triangle(5, wsi_ref.at[1], wso_ref[1])
    mo_ref[...] = mf[0:HEAD].astype(BF16)
    zo_ref[...] = zf[...].astype(BF16)


def solution(mesh):
    n = mesh.shape['dap']

    def local_step(msa, pair, msa_mask, res_mask, w_row_bias, w_row_in, w_row_out, w_col_in, w_col_out, w_opm_in, w_opm_out, w_ts_bias, w_ts_in, w_ts_out, w_te_bias, w_te_in, w_te_out):
        flat_in = lambda w: jnp.moveaxis(w, 1, -1).reshape(2, -1, w.shape[1])
        flat_out = lambda w: w.reshape(2, -1, w.shape[-1])
        args = (msa, pair, msa_mask.T, res_mask.reshape(1, -1),
                jnp.swapaxes(w_row_bias, 1, 2), flat_in(w_row_in), flat_out(w_row_out),
                flat_in(w_col_in), flat_out(w_col_out), flat_in(w_opm_in), flat_out(w_opm_out),
                jnp.swapaxes(w_ts_bias, 1, 2), flat_in(w_ts_in), flat_out(w_ts_out),
                jnp.swapaxes(w_te_bias, 1, 2), flat_in(w_te_in), flat_out(w_te_out))
        dma = pltpu.SemaphoreType.DMA

        def work_set(width, q_type):
            return [VMEM((2, width, SEQ), q_type), VMEM((2, SEQ, width), BF16), VMEM((2, width, SEQ), BF16),
                    VMEM((2, width, SEQ), F32), VMEM((2, width, SEQ), BF16)]
        flat = OWN * RES
        return pl.pallas_call(
            functools.partial(kernel, n),
            out_shape=(jax.ShapeDtypeStruct(msa.shape, BF16), jax.ShapeDtypeStruct(pair.shape, BF16)),
            in_specs=[pl.BlockSpec(memory_space=VMEM)] * len(args),
            out_specs=(pl.BlockSpec(memory_space=VMEM), pl.BlockSpec(memory_space=VMEM)),
            scratch_shapes=[
                VMEM((HEAD + 4, RES, SEQ), F32),
                VMEM((OWN, RES, LANE), F32),
                VMEM((OWN + 1, BLK, BLK, SEQ), BF16),
                VMEM((n, OWN, 2, BLK, SEQ), BF16),
                VMEM((2, n - 1, OWN, BLK, SEQ), BF16),
                VMEM((6, RES, LANE), BF16),
                VMEM((6, n, RES, LANE), BF16),
                VMEM((RES, flat), F32),
                VMEM((RES, SEQ), F32),
                VMEM((RES, SEQ), F32),
                VMEM((SEQ, RES), F32),
                VMEM((OWN, RES, LANE), F32),
                VMEM((RES, LANE), F32),
                VMEM((flat, flat), BF16),
                VMEM((flat, flat), BF16),
                VMEM((LANE, LANE), BF16),
                VMEM((SEQ, SEQ), BF16),
                VMEM((2, OWN // 2 + 1, WIDE, SEQ), BF16),
                VMEM((RES + OWN, WIDE), F32),
                VMEM((2, RES, WIDE), BF16),
                VMEM((2, n, RES, WIDE), BF16),
                VMEM((flat, WIDE), F32),
                VMEM((2, HEAD, SEQ), BF16),
                VMEM((2, LANE, SEQ), BF16),
                VMEM((WIDE, LANE), F32),
                VMEM((WIDE, LANE), BF16),
                VMEM((2, n, RES, LANE), BF16),
                VMEM((2, n, RES, LANE), BF16),
                *work_set(SEQ, BF16), *work_set(SEQ, F32), *work_set(LANE, F32),
                dma((6, n - 1)), dma((6, n)), dma((2,)), dma((2, OWN)), dma((2, n - 1)), dma((2, n)),
                dma((n - 1,)), dma((n,)), dma((2, n - 1)), dma((2, n)),
            ],
            compiler_params=pltpu.CompilerParams(
                collective_id=0, has_side_effects=True, vmem_limit_bytes=60 * WIDE * WIDE),
            name='evoformer',
        )(*args)

    in_specs = (P(('data', 'dap')), P(('data', 'dap')), P('data'), P('data')) + (P(),) * 13
    out_specs = (P(('data', 'dap')), P(('data', 'dap')))
    return jax.shard_map(local_step, mesh=mesh, in_specs=in_specs, out_specs=out_specs, check_vma=False)
```

profile of v0, /device:TPU:81, one launch (start us, length us, event | category | flops | bytes accessed | tf_op | source)
XLA Modules:
  0.0 108.6 jit_solution(15029039771960431639)
XLA Ops:
  0.6 105.0 %evoformer.1 = (bf16[32,64,256]{2,1,0:T(8,128)(2,1)}, bf16[8,64,128]{2,1,0:T(8,128)(2,1)}) custom-call(bf16[32,64,256]{2,1,0:T(8,128)(2,1)} %m_ref.1, bf16[8,64,128]{2,1,0:T(8,128)(2,1)} %z_ref.1, s32[64,256]{1,0:T(8,128)} %bitcast.32, s32[1,64]{1,0:T(1,128)} %bitcast.39, bf16[2,8,128]{2,1,0:T(8,128)(2,1)} %bitcast.36, bf16[2,1024,256]{2,1,0:T(8,128)(2,1)} %bitcast.25, ...), custom_call_target="tpu_custom_call" | custom-call | tf_op jit(solution)/shard_map/evoformer/pallas_call | solution.py:522
  105.6 0.0 copy-start
  105.6 2.3 %copy.21 = bf16[32,64,256]{2,1,0:T(8,128)(2,1)} copy(bf16[32,64,256]{2,1,0:T(8,128)(2,1)} %get-tuple-element.4) | data formatting | bytes 2097152
  108.0 0.0 copy-done
  108.0 0.7 copy.22
Async XLA Ops:
  105.6 2.4 %copy-start = (bf16[8,64,128]{2,1,0:T(8,128)(2,1)S(1)}, bf16[8,64,128]{2,1,0:T(8,128)(2,1)}, u32[]{:S(2)}) copy-start(bf16[8,64,128]{2,1,0:T(8,128)(2,1)} %get-tuple-element.5) | copy-start | bytes 393220
where the time goes:
time: 109 us
  Pallas kernels  105 us (96%)
  local copies, waits for them, and re-layouts  3 us (3%)
    pallas_call x1, Pallas kernels, local_step(): pl.pallas_call(functools.partial(kernel, n), out_shape=(jax.ShapeDtypeStr...  105 us
    unnamed x4, local copies, waits for them, and re-layouts  3 us

commit v1 on v0

--- a/solution.py
+++ b/solution.py
@@ -17,7 +17,8 @@
 SEQ = 2 * LANE
 WIDE = 4 * SEQ
 OWN = 8
-BLK = 16
+CHUNKS = 4
+EARLY = 2
 LOG2E = math.log2(math.e)
 NEG = -1e9 * LOG2E
 SCALE = HEAD ** -0.5 * LOG2E
@@ -89,7 +90,7 @@
     yield
 
 
-def col_attend(bufs, keep, ahead=2, late=1):
+def col_attend(bufs, keep, ahead=3, late=2):
     q, k, v, g, o = bufs
     heads, length = q.shape[0] // HEAD, q.shape[1]
     per = LANE // HEAD
@@ -166,32 +167,49 @@
         yield
 
 
-def kernel(n, m_ref, z_ref, mask_ref, res_ref,
-           wrb_ref, wri_ref, wro_ref, wci_ref, wco_ref, woi_ref, woo_ref,
-           wsb_ref, wsi_ref, wso_ref, web_ref, wei_ref, weo_ref,
-           mo_ref, zo_ref,
-           mf, zf, mcol, mrow, send_m, send_b, slot_b, bias_r, bias_t, mask_t, mask_n, rnorm, res_col,
+def kernel(n, inputs, *refs):
+    hbm, (mo_ref, zo_ref), held, sem_in = refs[:inputs], refs[inputs:inputs + 2], refs[inputs + 2:2 * inputs + 2], refs[2 * inputs + 2]
+    body(n, hbm, sem_in, mo_ref, zo_ref, *held, *refs[2 * inputs + 3:])
+
+
+def body(n, hbm, sem_in, mo_ref, zo_ref,
+         m_ref, z_ref, mask_ref, res_ref,
+         wrb_ref, wri_ref, wro_ref, wci_ref, wco_ref, woi_ref, woo_ref,
+         wsb_ref, wsi_ref, wso_ref, web_ref, wei_ref, weo_ref,
+         mf, zf, mcol, mrow, send_m, send_b, slot_b, bias_r, bias_t, mask_t, mask_n, rnorm, res_col,
            swap, rot, perm_s, perm_r, opm_rhs, opm_stage, opm_send, opm_all, opm_lhs, opm_w, opm_w4, opm_f, opm_t,
            send_z, slot_z,
            cq, ck, cv, cg, co, rq, rk, rv, rg, ro, tq, tk, tv, tg, to,
-           ss_b, rs_b, ss_m, rs_m, ss_c, rs_c, ss_r, rs_r, ss_z, rs_z):
+           ss_b, rs_b, ss_m, rs_m, rs_l, ss_c, rs_c, ss_r, rs_r, ss_z, rs_z):
+    held = (m_ref, z_ref, mask_ref, res_ref, wrb_ref, wri_ref, wro_ref, wci_ref, wco_ref, woi_ref, woo_ref,
+            wsb_ref, wsi_ref, wso_ref, web_ref, wei_ref, weo_ref)
+    loads = [(dst, pltpu.make_async_copy(src, dst, sem_in.at[i])) for i, (src, dst) in enumerate(zip(hbm, held))]
     me = lax.axis_index('dap')
     peers = [lax.rem(me + off, n) for off in range(1, n)]
     partner = me + 1 - 2 * lax.rem(me, 2)
-    others = [lax.rem(me + off, n) for off in range(2, n, 2)]
+    others = [lax.rem(me + off, n) for off in (2, n - 2, 4)]
     scope = jax.named_scope
 
     def remote(src, dst, send_sem, recv_sem, peer):
         return pltpu.make_async_remote_copy(src_ref=src, dst_ref=dst, send_sem=send_sem, recv_sem=recv_sem,
                                             device_id={'dap': peer}, device_id_type=pl.DeviceIdType.MESH)
+
+    def load_of(ref):
+        return next(c for dst, c in loads if dst is ref)
+
+    def need(*wanted):
+        for ref in wanted:
+            load_of(ref).wait()
 
     with scope('barrier'):
         barrier = pltpu.get_barrier_semaphore()
         for peer in peers:
             pl.semaphore_signal(barrier, inc=1, device_id={'dap': peer}, device_id_type=pl.DeviceIdType.MESH)
-        pl.semaphore_wait(barrier, n - 1)
-
-    def bias_send(idx, w_bias, heads):
+        order = (z_ref, wrb_ref, mask_ref, m_ref, wri_ref)
+        for ref in order + tuple(ref for ref in held if not any(ref is o for o in order)):
+            load_of(ref).start()
+
+    def bias_part(idx, w_bias, heads):
         z_cat = jnp.concatenate([layer_norm(zf[l]) for l in range(OWN)], axis=1)
         w = w_bias.astype(F32)
         w_rows = jnp.concatenate([jnp.broadcast_to(w[h:h + 1], (OWN, LANE)) for h in range(heads)], axis=0)
@@ -203,6 +221,12 @@
         part = part.astype(BF16)
         send_b[idx] = part
         slot_b[idx, me] = part
+
+    def bias_send(idx, w_bias, heads):
+        bias_part(idx, w_bias, heads)
+        bias_start(idx)
+
+    def bias_start(idx):
         for j, peer in enumerate(peers):
             remote(send_b.at[idx], slot_b.at[idx, me], ss_b.at[idx, j], rs_b.at[idx, me], peer).start()
 
@@ -218,40 +242,54 @@
         full = dot_tn(bias_slots(idx), swap[:, :heads * RES])
         out[...] = full[:RES] * LOG2E
 
-    def bias_key_local(idx, out):
-        full = dot_nn(swap[...], bias_slots(idx)) * LOG2E
+    def bias_key_local(idx, heads, out):
+        full = dot_nn(swap[:heads * RES, :], bias_slots(idx)) * LOG2E
         low = iota((RES, LANE), 1) < RES
-        for t in range(OWN // 2):
+        for t in range(heads // 2):
             lanes = slice(t * LANE, (t + 1) * LANE)
             out[:, lanes] = jnp.where(low, full[lanes][:RES], full[lanes][RES:])
 
-    row_bufs = lambda s: [buf.at[s] for buf in (rq, rk, rv, rg, ro)]
-
-    def row_pass(b, load, store, first, count, hook):
-        interleave(project(lambda: load(first), wri_ref.at[b], row_bufs(0)))
-        ro[1] = jnp.zeros(ro.shape[1:], BF16)
-
-        def finish(grp, slot, to):
+    GROUPS = OWN
+
+    def row_bufs(grp, slot):
+        return [buf.at[grp] for buf in (rq, rk, rv, rg)] + [ro.at[slot]]
+
+    def row_prepare(b, load):
+        ro[2:4] = jnp.zeros((2, SEQ, SEQ), BF16)
+
+        def body(half, carry):
+            parts = []
+            for j in range(GROUPS // 2):
+                grp = half * (GROUPS // 2) + j
+                parts.append(project(functools.partial(load, grp), wri_ref.at[b], row_bufs(grp, 0)))
+            interleave(*parts)
+            return carry
+        lax.fori_loop(0, 2, body, 0)
+
+    def row_pass(b, load, store, hook):
+        def finish(grp, slot):
             yield
             upd = dot_tn(ro[slot], wro_ref[b])
             yield
-            store(to, rounded(load(grp) + upd).reshape(4, RES, SEQ))
+            store(grp, rounded(load(grp) + upd).reshape(4, RES, SEQ))
             yield
 
         def body(step, carry):
-            grp = first + step
-            s = lax.rem(step, 2)
-            masks = [column(mask_t[...], me * HEAD + grp * 4 + j) for j in range(4)]
-            interleave(row_attend(row_bufs(s), bias_r, masks),
-                       project(lambda: load(jnp.minimum(grp + 1, first + count - 1)), wri_ref.at[b], row_bufs(1 - s)),
-                       finish(jnp.maximum(grp - 1, first), 1 - s, jnp.where(step == 0, OWN, grp - 1)))
+            s = lax.rem(step, 2) * 2
+            parts = []
+            for j in range(2):
+                grp = step * 2 + j
+                masks = [column(mask_t[...], me * HEAD + grp * 4 + r) for r in range(4)]
+                parts.append(row_attend(row_bufs(grp, s + j), bias_r, masks))
+                parts.append(finish(jnp.maximum(grp - 2, 0), 2 - s + j))
+            interleave(*parts)
             hook(step)
             return carry
-        lax.fori_loop(0, count, body, 0)
-        interleave(finish(first + count - 1, (count - 1) % 2, first + count - 1))
-
-    def triangle(idx, w_in, w_out):
-        bias_query_local(idx, 4, bias_t)
+        lax.fori_loop(0, GROUPS // 2, body, 0)
+        interleave(finish(GROUPS - 2, 2), finish(GROUPS - 1, 3))
+
+    def triangle(idx, w_in, w_out, assemble):
+        assemble(idx, 4, bias_t)
         with scope('tri'):
             masks = [res_col[:, 0:1]] * 4
             bufs = [[buf.at[c] for buf in (tq, tk, tv, tg, to)] for c in range(2)]
@@ -282,52 +320,66 @@
                 c.wait_recv()
         zf[...] = dot_nn(rot[...], jnp.concatenate([slot_z[idx, d] for d in range(n)], axis=0)).reshape(OWN, RES, LANE)
 
-    def opm_start(b):
-        out = dot_nn(selector(RES, RES, lambda r: r % OWN * OWN + r // OWN), opm_stage[0:RES].astype(BF16)).astype(BF16)
-        opm_send[b] = out
-        opm_all[b, me] = out
+    def partner_of(dev):
+        return dev + 1 - 2 * lax.rem(dev, 2)
+
+    def opm_start(b, half):
+        turn = selector(HEAD, HEAD, lambda r: r % 4 * OWN + r // 4)
+        out = dot_nn(turn, opm_stage[half * HEAD:(half + 1) * HEAD].astype(BF16)).astype(BF16)
+        opm_send[b, half] = out
+        opm_all[b, me, half] = out
         for j, peer in enumerate([partner] + others):
-            remote(opm_send.at[b], opm_all.at[b, me], ss_c.at[b, j], rs_c.at[b, me], peer).start()
-
-    def opm_forward(b):
+            remote(opm_send.at[b, half], opm_all.at[b, me, half], ss_c.at[b, half, j], rs_c.at[b, half, me], peer).start()
+
+    def opm_forward(b, half):
         with scope('opm_fwd'):
             for j, src in enumerate(others):
-                remote(opm_all.at[b, src], opm_all.at[b, src], ss_c.at[b, len(others) + 1 + j], rs_c.at[b, src], partner).wait_recv()
-                remote(opm_all.at[b, src], opm_all.at[b, src], ss_c.at[b, len(others) + 1 + j], rs_c.at[b, src], partner).start()
+                slot = opm_all.at[b, src, half]
+                c = remote(slot, slot, ss_c.at[b, half, len(others) + 1 + j], rs_c.at[b, half, src], partner)
+                c.wait_recv()
+                c.start()
 
     def opm_finish(b, w_out):
         with scope('opm_wait'):
-            for src in [partner] + [partner_of(o) for o in others]:
-                remote(opm_send.at[b], opm_all.at[b, src], ss_c.at[b, 0], rs_c.at[b, src], partner).wait_recv()
-            for j in range(n - 1):
-                remote(opm_send.at[b], opm_all.at[b, me], ss_c.at[b, j], rs_c.at[b, me], partner).wait_send()
+            for half in range(2):
+                for src in [partner] + [partner_of(o) for o in others]:
+                    slot = opm_all.at[b, src, half]
+                    remote(slot, slot, ss_c.at[b, half, 0], rs_c.at[b, half, src], partner).wait_recv()
+                for j in range(n - 1):
+                    slot = opm_send.at[b, half]
+                    remote(slot, slot, ss_c.at[b, half, j], rs_c.at[b, half, me], partner).wait_send()
         with scope('opm'):
             lhs = opm_all[b].reshape(OWN * RES, WIDE)
+            first = iota((n * 4, OWN, SEQ), 1) < 4
             for pair in range(OWN // 2):
-                part = rounded(dot_nn(lhs, opm_rhs[b, pair])).reshape(n, OWN, OWN, SEQ)
+                part = rounded(dot_nn(lhs, opm_rhs[b, pair])).reshape(n, 2, 4, OWN, SEQ)
+                h0, h1 = (part[:, half].reshape(n * 4, OWN, SEQ) for half in range(2))
+                turned = (jnp.where(first, h0, pltpu.roll(h1, 4, 1)), jnp.where(first, pltpu.roll(h0, 4, 1), h1))
                 for g in range(OWN):
-                    rows = part[:, g].reshape(RES, SEQ)
+                    rows = turned[g % 2].reshape(n, 4, OWN, SEQ)[:, g // 2].reshape(RES, SEQ)
                     for half in range(2):
                         l = pair * 2 + half
                         opm_lhs[l * RES:(l + 1) * RES, g * LANE:(g + 1) * LANE] = rows[:, half * LANE:(half + 1) * LANE]
             upd = dot_nn(opm_lhs[...].astype(BF16), w_out).reshape(OWN, RES, LANE)
             zf[...] = rounded(zf[...] + upd * rnorm[...])
 
-    def partner_of(dev):
-        return dev + 1 - 2 * lax.rem(dev, 2)
-
-    zf[...] = z_ref[...].astype(F32)
+    flat = OWN * RES
     with scope('bias0'):
-        bias_send(0, wrb_ref[0], OWN)
-
-    with scope('consts'):
-        flat = OWN * RES
+        need(z_ref, wrb_ref)
+        zf[...] = z_ref[...].astype(F32)
+        bias_part(0, wrb_ref[0], OWN)
         swap[...] = selector(flat, flat, lambda r: r // OWN % OWN * RES + r // RES * OWN + r % OWN)
+        perm_s[...] = selector(RES, RES, lambda r: r % OWN * OWN + r // OWN)
+        pl.semaphore_wait(barrier, n - 1)
+        bias_start(0)
+        need(mask_ref)
+        mask_t[...] = mask_ref[...].astype(F32)
+
+    def constants():
+        need(res_ref, woi_ref, woo_ref)
         rot[...] = selector(flat, flat, lambda r: r // OWN % OWN * RES + r % OWN * OWN + r // RES)
-        perm_s[...] = selector(LANE, LANE, lambda r: r % BLK * OWN + r // BLK)
         perm_r[...] = selector(SEQ, SEQ, lambda r: r % OWN * HEAD + r // OWN)
-        m_t = mask_ref[...].astype(F32)
-        mask_t[...] = m_t
+        m_t = mask_t[...]
         mask_n[...] = m_t.T
         norm = dot_nt(m_t.astype(BF16), m_t.astype(BF16))
         for l in range(OWN):
@@ -346,21 +398,30 @@
             opm_t[r * HEAD:(r + 1) * HEAD] = opm_f[pl.ds(r, HEAD, stride=HEAD), :].astype(BF16)
         co[1] = jnp.zeros(co.shape[1:], BF16)
 
-    bias_query_local(0, OWN, bias_r)
-
     def send_chunk(chunk):
-        rows = slice(chunk * BLK, (chunk + 1) * BLK)
-        for off in range(n):
-            dst = me if off == 0 else peers[off - 1]
-            blk = mf[rows, pl.ds(pl.multiple_of(dst * OWN, OWN), OWN), :].reshape(LANE, SEQ).astype(BF16)
-            blk = dot_nn(perm_s[...], blk).astype(BF16).reshape(OWN, BLK, SEQ)
-            if off == 0:
-                mcol[0:OWN, me * 2 + chunk] = blk
+        rows = pl.ds(pl.multiple_of(chunk * OWN, OWN), OWN)
+        dests = [me] + peers
+        blks = [mf[rows, pl.ds(pl.multiple_of(dst * OWN, OWN), OWN), :].reshape(RES, SEQ).astype(BF16) for dst in dests]
+        out = dot_nn(perm_s[...], jnp.concatenate(blks, axis=1))
+        mine = me * CHUNKS + chunk
+        for j in range(n):
+            blk = out[:, j * SEQ:(j + 1) * SEQ].reshape(OWN, OWN, SEQ).astype(BF16)
+            if j == 0:
+                mcol[0:OWN, mine] = blk
             else:
-                send_m[chunk, off - 1] = blk
-        for i in range(OWN):
+                send_m[chunk, j - 1] = blk
+        for j, peer in enumerate(peers):
+            remote(send_m.at[chunk, j, 0:EARLY], mcol.at[0:EARLY, mine], ss_m.at[0], rs_m.at[chunk], peer).start()
+
+    def send_rest():
+        for i in range(EARLY, OWN):
             for j, peer in enumerate(peers):
-                remote(send_m.at[chunk, j, i], mcol.at[i, me * 2 + chunk], ss_m.at[chunk], rs_m.at[chunk, i], peer).start()
+                remote(send_m.at[:, j, i], mcol.at[i, pl.ds(me * CHUNKS, CHUNKS)], ss_m.at[1], rs_l.at[i], peer).start()
+
+    def at(step, when, fn):
+        @pl.when(step == when)
+        def _():
+            fn()
 
     def load_first(grp):
         return m_ref[pl.ds(grp * 4, 4)].reshape(SEQ, SEQ).astype(F32)
@@ -368,21 +429,31 @@
     def store_first(grp, value):
         mf[pl.ds(grp * 4, 4)] = value
 
-    for chunk in range(2):
-        with scope('row1'):
-            row_pass(0, load_first, store_first, chunk * 4, 4, lambda step: None)
-        with scope('send_chunk'):
-            send_chunk(chunk)
+    with scope('prep1'):
+        need(m_ref, wri_ref)
+        row_prepare(0, load_first)
+    bias_query_local(0, OWN, bias_r)
+    with scope('row1'):
+        need(wro_ref)
+        def first_hook(step):
+            @pl.when(step > 0)
+            def _():
+                send_chunk(step - 1)
+        row_pass(0, load_first, store_first, first_hook)
+    with scope('send_chunk'):
+        send_chunk(CHUNKS - 1)
+        send_rest()
+    with scope('consts'):
+        constants()
 
     col_bufs = lambda s: [buf.at[s] for buf in (cq, ck, cv, cg, co)]
 
     def residue_wait(i):
-        for chunk in range(2):
-            seven = send_m.at[chunk, :, 0]
-            pltpu.make_async_copy(seven, seven, rs_m.at[chunk, i]).wait()
+        slot = send_m.at[:, :, 0]
+        pltpu.make_async_copy(slot, slot, rs_l.at[i]).wait()
 
     def load_col(i):
-        return mcol[i].reshape(SEQ, SEQ).astype(F32)
+        return mcol[i].astype(F32).reshape(SEQ, SEQ)
 
     def col_finish(b, i, slot):
         safe = jnp.minimum(i, OWN - 1)
@@ -390,7 +461,7 @@
         upd = dot_tn(co[slot], wco_ref[b])
         yield
         x = rounded(load_col(i) + upd)
-        mcol[i] = x.astype(BF16).reshape(BLK, BLK, SEQ)
+        mcol[i] = x.reshape(HEAD, OWN, SEQ).astype(BF16)
         x = layer_norm(x)
         yield
         local = (dot_nt(x, opm_w4[b]) * column(mask_n[...], me * OWN + safe)).astype(BF16)
@@ -405,33 +476,35 @@
         yield
 
     def send_back(i):
-        mrow[me, i] = mcol[i, pl.ds(me * 2, 2)]
+        mrow[me, i] = mcol[i, pl.ds(me * CHUNKS, CHUNKS)]
         for j, peer in enumerate(peers):
-            remote(mcol.at[i, pl.ds(peer * 2, 2)], mrow.at[me, i], ss_r.at[j], rs_r.at[me], peer).start()
-
+            remote(mcol.at[i, pl.ds(peer * CHUNKS, CHUNKS)], mrow.at[me, i], ss_r.at[j], rs_r.at[me], peer).start()
+
+    need(wsb_ref, wsi_ref, wso_ref, web_ref, wei_ref, weo_ref)
     with scope('col_first'):
-        residue_wait(0)
+        need(wci_ref, wco_ref)
+        for chunk in range(CHUNKS):
+            slot = send_m.at[chunk, :, 0:EARLY]
+            pltpu.make_async_copy(slot, slot, rs_m.at[chunk]).wait()
         interleave(project(lambda: load_col(0), wci_ref.at[0], col_bufs(0)))
 
-    def at(step, when, fn):
-        @pl.when(step == when)
-        def _():
-            fn()
-
     def stage_opm():
+        opm_forward(0, 1)
         opm_finish(0, opm_t[...])
         bias_send(1, wsb_ref[0], 4)
 
     def stage_start():
-        triangle(1, wsi_ref.at[0], wso_ref[0])
+        triangle(1, wsi_ref.at[0], wso_ref[0], bias_query_local)
         z_send(0)
+        bias_send(2, web_ref[0], 4)
 
     def stage_turn():
         z_recv(0)
-        bias_send(2, web_ref[0], 4)
+        triangle(2, wei_ref.at[0], weo_ref[0], bias_key_local)
+        bias_send(3, wrb_ref[1], OWN)
 
     def col_body(step, carry):
-        @pl.when(step < OWN - 1)
+        @pl.when(jnp.logical_and(step >= EARLY - 1, step < OWN - 1))
         def _():
             residue_wait(step + 1)
         with scope('col'):
@@ -443,62 +516,59 @@
                 project(lambda: load_col(lax.rem(nxt, OWN)), wci_ref.at[jnp.minimum(lax.div(nxt, OWN), 1)], col_bufs(1 - s)),
                 col_finish(jnp.where(prev >= OWN, 1, 0), jnp.where(step == 0, OWN, lax.rem(jnp.maximum(prev, 0), OWN)), 1 - s))
 
+        at(step, 4, lambda: opm_start(0, 0))
+        at(step, OWN, lambda: opm_start(0, 1))
+        at(step, OWN, lambda: opm_forward(0, 0))
+        at(step, OWN + 3, stage_opm)
+        at(step, OWN + 4, lambda: opm_start(1, 0))
+        at(step, OWN + 5, stage_start)
+        at(step, OWN + 7, stage_turn)
+
         @pl.when(prev >= OWN)
         def _():
             send_back(prev - OWN)
-        at(step, OWN, lambda: opm_start(0))
-        at(step, OWN + 2, lambda: opm_forward(0))
-        at(step, OWN + 3, stage_opm)
-        at(step, OWN + 5, stage_start)
-        at(step, OWN + 7, stage_turn)
         return carry
     lax.fori_loop(0, 2 * OWN, col_body, 0)
     with scope('col_last'):
         interleave(col_finish(1, OWN - 1, 1))
+        opm_start(1, 1)
         send_back(OWN - 1)
-
-    triangle(2, wei_ref.at[0], weo_ref[0])
-    with scope('bias3'):
-        bias_send(3, wrb_ref[1], OWN)
-        opm_start(1)
-
+    opm_forward(1, 0)
+
+    opm_forward(1, 1)
+    opm_finish(1, woo_ref[1])
+    with scope('bias4'):
+        bias_send(4, web_ref[1], 4)
     with scope('m_wait'):
-        for chunk in range(2):
-            sent = send_m.at[chunk]
-            pltpu.make_async_copy(sent, sent, ss_m.at[chunk]).wait()
+        for half in range(2):
+            sent = send_m.at[:, :, 0:EARLY] if half == 0 else send_m.at[:, :, EARLY:OWN]
+            pltpu.make_async_copy(sent, sent, ss_m.at[half]).wait()
         for j, src in enumerate(peers):
             pltpu.make_async_copy(mrow.at[src], mrow.at[src], rs_r.at[src]).wait()
             pltpu.make_async_copy(mrow.at[src], mrow.at[src], ss_r.at[j]).wait()
     with scope('m_perm'):
         for d in range(n):
-            mf[0:HEAD, d * OWN:(d + 1) * OWN, :] = dot_nn(perm_r[...], mrow[d].reshape(SEQ, SEQ)).reshape(HEAD, OWN, SEQ)
-    bias_key_local(3, bias_r)
-
-    def stage_opm2():
-        opm_finish(1, woo_ref[1])
-        bias_send(4, web_ref[1], 4)
-
-    def stage_end2():
-        triangle(4, wei_ref.at[1], weo_ref[1])
-        z_send(1)
-
-    def stage_turn2():
-        z_recv(1)
-        bias_send(5, wsb_ref[1], 4)
-
-    def row_hook(step):
-        at(step, 2, lambda: opm_forward(1))
-        at(step, 3, stage_opm2)
-        at(step, 5, stage_end2)
-        at(step, 7, stage_turn2)
+            mf[:, d * OWN:(d + 1) * OWN, :] = dot_nn(perm_r[...], mrow[d].astype(F32).reshape(SEQ, SEQ).astype(BF16)).reshape(HEAD, OWN, SEQ)
 
     def load_second(grp):
         return mf[pl.ds(grp * 4, 4)].reshape(SEQ, SEQ)
 
+    def store_second(grp, value):
+        mo_ref[pl.ds(grp * 4, 4)] = value.astype(BF16)
+
+    with scope('prep2'):
+        row_prepare(1, load_second)
+    bias_key_local(3, OWN, bias_r)
+
+    def stage_end2():
+        triangle(4, wei_ref.at[1], weo_ref[1], bias_query_local)
+        z_send(1)
+        bias_send(5, wsb_ref[1], 4)
+
     with scope('row2'):
-        row_pass(1, load_second, store_first, 0, OWN, row_hook)
-    triangle(5, wsi_ref.at[1], wso_ref[1])
-    mo_ref[...] = mf[0:HEAD].astype(BF16)
+        row_pass(1, load_second, store_second, lambda step: at(step, 2, stage_end2))
+    z_recv(1)
+    triangle(5, wsi_ref.at[1], wso_ref[1], bias_key_local)
     zo_ref[...] = zf[...].astype(BF16)
 
 
@@ -515,21 +585,22 @@
                 jnp.swapaxes(w_te_bias, 1, 2), flat_in(w_te_in), flat_out(w_te_out))
         dma = pltpu.SemaphoreType.DMA
 
-        def work_set(width, q_type):
-            return [VMEM((2, width, SEQ), q_type), VMEM((2, SEQ, width), BF16), VMEM((2, width, SEQ), BF16),
-                    VMEM((2, width, SEQ), F32), VMEM((2, width, SEQ), BF16)]
+        def work_set(slots, width, q_type, outs=2):
+            return [VMEM((slots, width, SEQ), q_type), VMEM((slots, SEQ, width), BF16), VMEM((slots, width, SEQ), BF16),
+                    VMEM((slots, width, SEQ), F32), VMEM((outs, width, SEQ), BF16)]
         flat = OWN * RES
         return pl.pallas_call(
-            functools.partial(kernel, n),
+            functools.partial(kernel, n, len(args)),
             out_shape=(jax.ShapeDtypeStruct(msa.shape, BF16), jax.ShapeDtypeStruct(pair.shape, BF16)),
-            in_specs=[pl.BlockSpec(memory_space=VMEM)] * len(args),
+            in_specs=[pl.BlockSpec(memory_space=pl.ANY)] * len(args),
             out_specs=(pl.BlockSpec(memory_space=VMEM), pl.BlockSpec(memory_space=VMEM)),
             scratch_shapes=[
-                VMEM((HEAD + 4, RES, SEQ), F32),
+                *[VMEM(a.shape, a.dtype) for a in args], dma((len(args),)),
+                VMEM((HEAD, RES, SEQ), F32),
                 VMEM((OWN, RES, LANE), F32),
-                VMEM((OWN + 1, BLK, BLK, SEQ), BF16),
-                VMEM((n, OWN, 2, BLK, SEQ), BF16),
-                VMEM((2, n - 1, OWN, BLK, SEQ), BF16),
+                VMEM((OWN + 1, HEAD, OWN, SEQ), BF16),
+                VMEM((n, OWN, CHUNKS, OWN, SEQ), BF16),
+                VMEM((CHUNKS, n - 1, OWN, OWN, SEQ), BF16),
                 VMEM((6, RES, LANE), BF16),
                 VMEM((6, n, RES, LANE), BF16),
                 VMEM((RES, flat), F32),
@@ -540,12 +611,12 @@
                 VMEM((RES, LANE), F32),
                 VMEM((flat, flat), BF16),
                 VMEM((flat, flat), BF16),
-                VMEM((LANE, LANE), BF16),
+                VMEM((RES, RES), BF16),
                 VMEM((SEQ, SEQ), BF16),
                 VMEM((2, OWN // 2 + 1, WIDE, SEQ), BF16),
                 VMEM((RES + OWN, WIDE), F32),
-                VMEM((2, RES, WIDE), BF16),
-                VMEM((2, n, RES, WIDE), BF16),
+                VMEM((2, 2, HEAD, WIDE), BF16),
+                VMEM((2, n, 2, HEAD, WIDE), BF16),
                 VMEM((flat, WIDE), F32),
                 VMEM((2, HEAD, SEQ), BF16),
                 VMEM((2, LANE, SEQ), BF16),
@@ -553,8 +624,8 @@
                 VMEM((WIDE, LANE), BF16),
                 VMEM((2, n, RES, LANE), BF16),
                 VMEM((2, n, RES, LANE), BF16),
-                *work_set(SEQ, BF16), *work_set(SEQ, F32), *work_set(LANE, F32),
-                dma((6, n - 1)), dma((6, n)), dma((2,)), dma((2, OWN)), dma((2, n - 1)), dma((2, n)),
+                *work_set(2, SEQ, BF16), *work_set(OWN, SEQ, F32, 4), *work_set(2, LANE, F32),
+                dma((6, n - 1)), dma((6, n)), dma((2,)), dma((CHUNKS,)), dma((OWN,)), dma((2, 2, n - 1)), dma((2, 2, n)),
                 dma((n - 1,)), dma((n,)), dma((2, n - 1)), dma((2, n)),
             ],
             compiler_params=pltpu.CompilerParams(

time: 109 us -> 89.2 us (0.82)
  Pallas kernels: 105 us -> 85.5 us
    pallas_call x1, Pallas kernels: 105 us -> 85.5 us  [local_step(): pl.pallas_call(functools.partial(kernel, n, len(args)), out_shape=(jax.Sh...]
where the time goes in v1:
time: 89.2 us; the launch traced here: 89.1 us
  Pallas kernels  85.5 us (96%)
  local copies, waits for them, and re-layouts  3 us (3%)
    pallas_call x1, Pallas kernels, local_step(): pl.pallas_call(functools.partial(kernel, n, len(args)), out_shape=(jax.Sh...  85.5 us
    unnamed x4, local copies, waits for them, and re-layouts  3 us

profile of v1, /device:TPU:81, one launch (start us, length us, event | category | flops | bytes accessed | tf_op | source)
XLA Modules:
  0.0 89.1 jit_solution(8728373424764939865)
XLA Ops:
  0.6 85.5 %evoformer.1 = (bf16[32,64,256]{2,1,0:T(8,128)(2,1)}, bf16[8,64,128]{2,1,0:T(8,128)(2,1)}) custom-call(bf16[32,64,256]{2,1,0:T(8,128)(2,1)} %refs_0_.1, bf16[8,64,128]{2,1,0:T(8,128)(2,1)} %refs_1_.1, s32[64,256]{1,0:T(8,128)} %bitcast.32, s32[1,64]{1,0:T(1,128)} %bitcast.39, bf16[2,8,128]{2,1,0:T(8,128)(2,1)} %bitcast.36, bf16[2,1024,256]{2,1,0:T(8,128)(2,1)} %bitcast.25, ...), custom_call_target="tpu_custom_call" | custom-call | tf_op jit(solution)/shard_map/evoformer/pallas_call | solution.py:592
  86.1 0.0 copy-start
  86.1 2.3 %copy.21 = bf16[32,64,256]{2,1,0:T(8,128)(2,1)} copy(bf16[32,64,256]{2,1,0:T(8,128)(2,1)} %get-tuple-element.4) | data formatting | bytes 2097152
  88.5 0.0 copy-done
  88.5 0.7 copy.22
Async XLA Ops:
  86.1 2.4 %copy-start = (bf16[8,64,128]{2,1,0:T(8,128)(2,1)S(1)}, bf16[8,64,128]{2,1,0:T(8,128)(2,1)}, u32[]{:S(2)}) copy-start(bf16[8,64,128]{2,1,0:T(8,128)(2,1)} %get-tuple-element.5) | copy-start | bytes 393220

commit v2 on v1

--- a/solution.py
+++ b/solution.py
@@ -498,11 +498,6 @@
         z_send(0)
         bias_send(2, web_ref[0], 4)
 
-    def stage_turn():
-        z_recv(0)
-        triangle(2, wei_ref.at[0], weo_ref[0], bias_key_local)
-        bias_send(3, wrb_ref[1], OWN)
-
     def col_body(step, carry):
         @pl.when(jnp.logical_and(step >= EARLY - 1, step < OWN - 1))
         def _():
@@ -519,10 +514,9 @@
         at(step, 4, lambda: opm_start(0, 0))
         at(step, OWN, lambda: opm_start(0, 1))
         at(step, OWN, lambda: opm_forward(0, 0))
-        at(step, OWN + 3, stage_opm)
+        at(step, OWN + 4, stage_opm)
         at(step, OWN + 4, lambda: opm_start(1, 0))
-        at(step, OWN + 5, stage_start)
-        at(step, OWN + 7, stage_turn)
+        at(step, OWN + 6, stage_start)
 
         @pl.when(prev >= OWN)
         def _():
@@ -531,14 +525,15 @@
     lax.fori_loop(0, 2 * OWN, col_body, 0)
     with scope('col_last'):
         interleave(col_finish(1, OWN - 1, 1))
+        send_back(OWN - 1)
         opm_start(1, 1)
-        send_back(OWN - 1)
+
+    z_recv(0)
+    triangle(2, wei_ref.at[0], weo_ref[0], bias_key_local)
+
+    with scope('bias3'):
+        bias_send(3, wrb_ref[1], OWN)
     opm_forward(1, 0)
-
-    opm_forward(1, 1)
-    opm_finish(1, woo_ref[1])
-    with scope('bias4'):
-        bias_send(4, web_ref[1], 4)
     with scope('m_wait'):
         for half in range(2):
             sent = send_m.at[:, :, 0:EARLY] if half == 0 else send_m.at[:, :, EARLY:OWN]
@@ -558,6 +553,10 @@
 
     with scope('prep2'):
         row_prepare(1, load_second)
+    opm_forward(1, 1)
+    opm_finish(1, woo_ref[1])
+    with scope('bias4'):
+        bias_send(4, web_ref[1], 4)
     bias_key_local(3, OWN, bias_r)
 
     def stage_end2():

time: 89.2 us -> 83.6 us (0.937)
  Pallas kernels: 85.5 us -> 79.9 us
    pallas_call x1, Pallas kernels: 85.5 us -> 79.9 us  [local_step(): pl.pallas_call(functools.partial(kernel, n, len(args)), out_shape=(jax.Sh...]
where the time goes in v2:
time: 83.6 us; the launch traced here: 83.5 us
  Pallas kernels  79.9 us (96%)
  local copies, waits for them, and re-layouts  3 us (4%)
    pallas_call x1, Pallas kernels, local_step(): pl.pallas_call(functools.partial(kernel, n, len(args)), out_shape=(jax.Sh...  79.9 us
    unnamed x4, local copies, waits for them, and re-layouts  3 us

profile of v2, /device:TPU:81, one launch (start us, length us, event | category | flops | bytes accessed | tf_op | source)
XLA Modules:
  0.0 83.5 jit_solution(2861615701929181710)
XLA Ops:
  0.6 79.9 %evoformer.1 = (bf16[32,64,256]{2,1,0:T(8,128)(2,1)}, bf16[8,64,128]{2,1,0:T(8,128)(2,1)}) custom-call(bf16[32,64,256]{2,1,0:T(8,128)(2,1)} %refs_0_.1, bf16[8,64,128]{2,1,0:T(8,128)(2,1)} %refs_1_.1, s32[64,256]{1,0:T(8,128)} %bitcast.32, s32[1,64]{1,0:T(1,128)} %bitcast.39, bf16[2,8,128]{2,1,0:T(8,128)(2,1)} %bitcast.36, bf16[2,1024,256]{2,1,0:T(8,128)(2,1)} %bitcast.25, ...), custom_call_target="tpu_custom_call" | custom-call | tf_op jit(solution)/shard_map/evoformer/pallas_call | solution.py:591
  80.5 0.0 copy-start
  80.5 2.3 %copy.21 = bf16[32,64,256]{2,1,0:T(8,128)(2,1)} copy(bf16[32,64,256]{2,1,0:T(8,128)(2,1)} %get-tuple-element.4) | data formatting | bytes 2097152
  82.9 0.0 copy-done
  82.9 0.7 copy.22
Async XLA Ops:
  80.5 2.4 %copy-start = (bf16[8,64,128]{2,1,0:T(8,128)(2,1)S(1)}, bf16[8,64,128]{2,1,0:T(8,128)(2,1)}, u32[]{:S(2)}) copy-start(bf16[8,64,128]{2,1,0:T(8,128)(2,1)} %get-tuple-element.5) | copy-start | bytes 393220

commit v3 on v2

--- a/solution.py
+++ b/solution.py
@@ -90,7 +90,7 @@
     yield
 
 
-def col_attend(bufs, keep, ahead=3, late=2):
+def col_attend(bufs, keep, ahead=4, late=2):
     q, k, v, g, o = bufs
     heads, length = q.shape[0] // HEAD, q.shape[1]
     per = LANE // HEAD
@@ -168,15 +168,15 @@
 
 
 def kernel(n, inputs, *refs):
-    hbm, (mo_ref, zo_ref), held, sem_in = refs[:inputs], refs[inputs:inputs + 2], refs[inputs + 2:2 * inputs + 2], refs[2 * inputs + 2]
-    body(n, hbm, sem_in, mo_ref, zo_ref, *held, *refs[2 * inputs + 3:])
-
-
-def body(n, hbm, sem_in, mo_ref, zo_ref,
+    hbm, outs, held, sem_in = refs[:inputs], refs[inputs:inputs + 2], refs[inputs + 2:2 * inputs + 2], refs[2 * inputs + 2]
+    body(n, hbm, sem_in, outs, *held, *refs[2 * inputs + 3:])
+
+
+def body(n, hbm, sem_in, outs,
          m_ref, z_ref, mask_ref, res_ref,
          wrb_ref, wri_ref, wro_ref, wci_ref, wco_ref, woi_ref, woo_ref,
          wsb_ref, wsi_ref, wso_ref, web_ref, wei_ref, weo_ref,
-         mf, zf, mcol, mrow, send_m, send_b, slot_b, bias_r, bias_t, mask_t, mask_n, rnorm, res_col,
+         mo, zo, sem_out, mf, zf, mcol, mrow, send_m, send_b, slot_b, bias_r, bias_t, mask_t, mask_n, rnorm, res_col,
            swap, rot, perm_s, perm_r, opm_rhs, opm_stage, opm_send, opm_all, opm_lhs, opm_w, opm_w4, opm_f, opm_t,
            send_z, slot_z,
            cq, ck, cv, cg, co, rq, rk, rv, rg, ro, tq, tk, tv, tg, to,
@@ -549,7 +549,7 @@
         return mf[pl.ds(grp * 4, 4)].reshape(SEQ, SEQ)
 
     def store_second(grp, value):
-        mo_ref[pl.ds(grp * 4, 4)] = value.astype(BF16)
+        mo[pl.ds(grp * 4, 4)] = value.astype(BF16)
 
     with scope('prep2'):
         row_prepare(1, load_second)
@@ -566,9 +566,14 @@
 
     with scope('row2'):
         row_pass(1, load_second, store_second, lambda step: at(step, 2, stage_end2))
+    finals = [pltpu.make_async_copy(src, dst, sem_out.at[i]) for i, (src, dst) in enumerate(zip((mo, zo), outs))]
+    finals[0].start()
     z_recv(1)
     triangle(5, wsi_ref.at[1], wso_ref[1], bias_key_local)
-    zo_ref[...] = zf[...].astype(BF16)
+    zo[...] = zf[...].astype(BF16)
+    finals[1].start()
+    for copy in finals:
+        copy.wait()
 
 
 def solution(mesh):
@@ -592,9 +597,10 @@
             functools.partial(kernel, n, len(args)),
             out_shape=(jax.ShapeDtypeStruct(msa.shape, BF16), jax.ShapeDtypeStruct(pair.shape, BF16)),
             in_specs=[pl.BlockSpec(memory_space=pl.ANY)] * len(args),
-            out_specs=(pl.BlockSpec(memory_space=VMEM), pl.BlockSpec(memory_space=VMEM)),
+            out_specs=(pl.BlockSpec(memory_space=pl.ANY), pl.BlockSpec(memory_space=pl.ANY)),
             scratch_shapes=[
                 *[VMEM(a.shape, a.dtype) for a in args], dma((len(args),)),
+                VMEM(msa.shape, BF16), VMEM(pair.shape, BF16), dma((2,)),
                 VMEM((HEAD, RES, SEQ), F32),
                 VMEM((OWN, RES, LANE), F32),
                 VMEM((OWN + 1, HEAD, OWN, SEQ), BF16),

time: 83.6 us -> 83.2 us (level)
  no operation moved by 1% of the time
where the time goes in v3:
time: 83.2 us; the launch traced here: 83.1 us
  Pallas kernels  79.4 us (95%)
  local copies, waits for them, and re-layouts  3 us (4%)
    pallas_call x1, Pallas kernels, local_step(): pl.pallas_call(functools.partial(kernel, n, len(args)), out_shape=(jax.Sh...  79.4 us
    unnamed x4, local copies, waits for them, and re-layouts  3 us

profile of v3, /device:TPU:81, one launch (start us, length us, event | category | flops | bytes accessed | tf_op | source)
XLA Modules:
  0.0 83.1 jit_solution(3931966602012002403)
XLA Ops:
  0.6 79.4 %evoformer.1 = (bf16[32,64,256]{2,1,0:T(8,128)(2,1)}, bf16[8,64,128]{2,1,0:T(8,128)(2,1)}) custom-call(bf16[32,64,256]{2,1,0:T(8,128)(2,1)} %refs_0_.1, bf16[8,64,128]{2,1,0:T(8,128)(2,1)} %refs_1_.1, s32[64,256]{1,0:T(8,128)} %bitcast.32, s32[1,64]{1,0:T(1,128)} %bitcast.39, bf16[2,8,128]{2,1,0:T(8,128)(2,1)} %bitcast.36, bf16[2,1024,256]{2,1,0:T(8,128)(2,1)} %bitcast.25, ...), custom_call_target="tpu_custom_call" | custom-call | tf_op jit(solution)/shard_map/evoformer/pallas_call | solution.py:596
  80.1 0.0 copy-start
  80.1 2.3 %copy.21 = bf16[32,64,256]{2,1,0:T(8,128)(2,1)} copy(bf16[32,64,256]{2,1,0:T(8,128)(2,1)} %get-tuple-element.4) | data formatting | bytes 2097152
  82.4 0.0 copy-done
  82.4 0.7 copy.22
Async XLA Ops:
  80.1 2.4 %copy-start = (bf16[8,64,128]{2,1,0:T(8,128)(2,1)S(1)}, bf16[8,64,128]{2,1,0:T(8,128)(2,1)}, u32[]{:S(2)}) copy-start(bf16[8,64,128]{2,1,0:T(8,128)(2,1)} %get-tuple-element.5) | copy-start | bytes 393220
